TPU v7x, 32 devices: a 4x2x2 block of a 4x4x8 slice. The times are simulated.
32 devices in a mesh: dp: 4 (over y, z), tp: 8 (over x, core).
Axes of the slice: x: 4, y: 2, z: 2, core: 2. Of those that a mesh axis runs over, the one named last changes fastest.
The devices are a block of a 4x4x8 slice.
Arguments:
- hidden: bfloat16 [4, 256, 5120], P('dp', 'tp'), parts along dimension 0
- ln1_gain: float32 [5120], replicated
- ln1_bias: float32 [5120], replicated
- w_qkv: bfloat16 [5120, 3, 40, 128], P(None, None, 'tp')
- b_qkv: bfloat16 [3, 40, 128], P(None, 'tp')
- w_out: bfloat16 [40, 128, 5120], P('tp')
- b_out: bfloat16 [5120], replicated
- ln2_gain: float32 [5120], replicated
- ln2_bias: float32 [5120], replicated
- w_up: bfloat16 [5120, 20480], P(None, 'tp')
- b_up: bfloat16 [20480], P('tp')
- w_down: bfloat16 [20480, 5120], P('tp')
- b_down: bfloat16 [5120], replicated
Outputs:
- output: bfloat16 [4, 256, 5120], P('dp', 'tp'), parts along dimension 0
There are 4 independent parts. A program takes and returns all parts, laid end to end along the dimension named above; an argument that names none is the same for every part.
All inputs are finite; a program needn't handle non-finite values.
Results may differ from a plain program's by a relative error of at most 0.010208.
Values are sent between devices in bfloat16 or wider.
A program may use at most 768 MiB of HBM per device.

v0:
```python
import functools

import jax
import jax.numpy as jnp
from jax import lax
from jax.experimental import pallas as pl
from jax.experimental.pallas import tpu as pltpu
from jax.sharding import PartitionSpec as P

LN_EPS = 1e-5
MESH = pl.DeviceIdType.MESH
CH = 512
GATHER_QKV = (5, 4, 5)
GATHER_UP = (5, 4, 5)
LAGS_OUT = (2, 6, 11)
LAGS_DOWN = (2, 6, 10)
N_FAR = 1
N_WD = 4


def f32(v):
    return v.astype(jnp.float32)


def bf16(v):
    return v.astype(jnp.bfloat16)


def dot(a, b):
    return jnp.dot(a, b, preferred_element_type=jnp.float32)


def layer_kernel(
    n_dev,
    x_hbm, g1_hbm, s1_hbm, wqkv, bqkv_hbm, wo, bo_hbm, g2_hbm, s2_hbm, wu, bu_hbm, wd, bd_hbm,
    out_ref,
    x_ref, g1_ref, s1_ref, g2_ref, s2_ref, bqkv_ref, bo_ref, bu_ref, bd_ref,
    xb, h_all, u_w, pool, acc, qkv, ctx, act, psend, precv,
    hop_s, hop_r, fin_s, fin_r, x1,
    xsem, psem, usem, osem, dsem, ag_send, ag_l, ag_r, ag_l2, ag_r2, ag_p,
    rs_send, rs_p, rs_hl, rs_hr, rs_fl, rs_fr,
):
    small = [pltpu.make_async_copy(a, b, xsem.at[i]) for i, (a, b) in enumerate(
        ((x_hbm, x_ref), (g1_hbm, g1_ref), (s1_hbm, s1_ref)))]
    late = [pltpu.make_async_copy(a, b, psem.at[i]) for i, (a, b) in enumerate(
        ((bqkv_hbm, bqkv_ref), (bo_hbm, bo_ref), (g2_hbm, g2_ref), (s2_hbm, s2_ref), (bu_hbm, bu_ref), (bd_hbm, bd_ref)))]
    for copy in small + late:
        copy.start()
    n_chips = n_dev // 2
    rows, dim = x_ref.shape
    nch = dim // CH
    ng = nch // 2
    hr = rows // 2
    side = hr * n_chips
    st_rows = 2 * side
    n_tok = 2 * st_rows
    hc = CH // 2
    n_slab = wqkv.shape[0]
    hd = wqkv.shape[2]
    heads = n_slab // 3
    qw = n_slab * hd
    ff = wu.shape[1]
    nt = ff // CH
    me = lax.axis_index("tp")
    chip, core = me // 2, me % 2
    right = {"tp": ((chip + 1) % n_chips) * 2 + core}
    left = {"tp": ((chip + n_chips - 1) % n_chips) * 2 + core}
    mate = {"tp": chip * 2 + (1 - core)}
    far = {"tp": ((chip + 2) % n_chips) * 2 + core}

    def push(src, dst, ssem, rsem, dev):
        return pltpu.make_async_remote_copy(
            src_ref=src, dst_ref=dst, send_sem=ssem, recv_sem=rsem, device_id=dev, device_id_type=MESH)

    barrier = pltpu.get_barrier_semaphore()
    for dev in (left, right, mate, far):
        pl.semaphore_signal(barrier, inc=1, device_id=dev, device_id_type=MESH)

    def load_qkv(j):
        for s in range(n_slab):
            pltpu.make_async_copy(
                wqkv.at[s, pl.ds(pl.multiple_of(j * CH, CH), CH), :],
                u_w.at[j, :, pl.ds(s * hd, hd)], usem.at[j]).start()

    def load_up(j):
        return pltpu.make_async_copy(
            wu.at[pl.ds(pl.multiple_of(j * CH, CH), CH), :], u_w.at[j], usem.at[j])

    kt = heads * hd
    nk = ff // kt
    o_base = (N_WD - 1) * nk

    def load_down(q):
        g, slot = q % ng, q % N_WD
        for k in range(nk):
            pltpu.make_async_copy(
                wd.at[pl.ds(k * kt, kt), pl.ds(pl.multiple_of(g * 2 * CH, 2 * CH), 2 * CH)],
                pool.at[slot * nk + k], dsem.at[slot]).start()

    def wait_down(q):
        slot = q % N_WD
        pltpu.make_async_copy(pool.at[pl.ds(slot * nk, nk)], pool.at[pl.ds(slot * nk, nk)], dsem.at[slot]).wait()

    def init_loads(j, c):
        load_qkv(j)
        return c

    lax.fori_loop(0, nch, init_loads, 0)
    for g in range(ng):
        pltpu.make_async_copy(wo.at[:, pl.ds(g * 2 * CH, 2 * CH)], pool.at[o_base + g], osem).start()
    for q in range(N_WD - 1):
        load_down(q)

    def norm(get, put, n, gain_ref, shift_ref):
        tot = jnp.zeros((n, CH), jnp.float32)
        for j in range(nch):
            tot += get(j)
        mean = jnp.sum(tot, axis=1, keepdims=True) * (1.0 / dim)
        tot = jnp.zeros((n, CH), jnp.float32)
        for j in range(nch):
            cen = get(j) - mean
            tot += cen * cen
        var = jnp.sum(tot, axis=1, keepdims=True) * (1.0 / dim)
        inv = lax.rsqrt(var + LN_EPS)
        for j in range(nch):
            cols = slice(j * CH, (j + 1) * CH)
            put(j, bf16((get(j) - mean) * inv * gain_ref[:, cols] + shift_ref[:, cols]))

    def put_both(j, y):
        h_all[j, 0, 0:hr, :] = y[0:hr]
        h_all[j, 1, 0:hr, :] = y[hr:]

    def put_stream(st):
        def put(j, y):
            h_all[j, st, 0:hr, :] = y
        return put

    for copy in small:
        copy.wait()
    norm(lambda j: f32(x_ref[:, j * CH:(j + 1) * CH]), put_both, rows, g1_ref, s1_ref)
    acc[...] = jnp.zeros_like(acc)
    pl.semaphore_wait(barrier, 4)

    def piece_both(v, s, r, lo=0, n=CH):
        return h_all.at[v, :, pl.ds(s * side + r * hr, hr), pl.ds(lo, n)]

    def all_both(v, s):
        return h_all.at[v, :, pl.ds(s * side, side), :]

    def piece_stream(v, s, r, lo=0, n=CH):
        return h_all.at[pl.ds((v % ng) * 2, 2), v // ng, pl.ds(s * side + r * hr, hr), pl.ds(lo, n)]

    def all_stream(v, s):
        return h_all.at[pl.ds((v % ng) * 2, 2), v // ng, pl.ds(s * side, side), :]

    def send_own(at, v):
        push(at(v, 0, 0), at(v, 0, 3), ag_send, ag_l.at[v], right).start()
        push(at(v, 0, 0), at(v, 0, 1), ag_send, ag_r.at[v], left).start()
        push(at(v, 0, 0), at(v, 1, 0), ag_send, ag_p.at[v], mate).start()

    def wait_mate(whole, v):
        push(whole(v, 0), whole(v, 1), ag_send, ag_p.at[v], mate).wait_recv()

    def forward_one(at, i):
        with jax.named_scope("gw1l"):
            push(at(i, 0, 0), at(i, 0, 3), ag_send, ag_l.at[i], right).wait_recv()
        push(at(i, 0, 3, 0, hc), at(i, 0, 2, 0, hc), ag_send, ag_l2.at[i], right).start()
        with jax.named_scope("gw1r"):
            push(at(i, 0, 0), at(i, 0, 1), ag_send, ag_r.at[i], left).wait_recv()
        push(at(i, 0, 1, hc, hc), at(i, 0, 2, hc, hc), ag_send, ag_r2.at[i], left).start()
        push(at(i, 0, 3), at(i, 1, 3), ag_send, ag_p.at[i], mate).start()
        push(at(i, 0, 1), at(i, 1, 1), ag_send, ag_p.at[i], mate).start()

    def forward_two(at, j):
        with jax.named_scope("gw2"):
            push(at(j, 0, 3, 0, hc), at(j, 0, 2, 0, hc), ag_send, ag_l2.at[j], right).wait_recv()
            push(at(j, 0, 1, hc, hc), at(j, 0, 2, hc, hc), ag_send, ag_r2.at[j], left).wait_recv()
        push(at(j, 0, 2), at(j, 1, 2), ag_send, ag_p.at[j], mate).start()

    def gather(at, whole, n_use, consume, lags):
        look, lag_b, lag_c = lags

        def step(i, c):
            @pl.when(i < nch)
            def _():
                forward_one(at, i)

            @pl.when(i + look < nch)
            def _():
                send_own(at, i + look)

            @pl.when((i >= lag_b) & (i < nch + lag_b))
            def _():
                forward_two(at, i - lag_b)

            @pl.when(i >= lag_c)
            def _():
                j = i - lag_c
                with jax.named_scope("gwp"):
                    wait_mate(whole, j)
                with jax.named_scope("guse"):
                    consume(j)
            return c

        lax.fori_loop(0, n_use + lag_c, step, 0)

    def gather_drain():
        sent = h_all.at[:, :, pl.ds(0, 7 * hr), :]
        push(sent, sent, ag_send, ag_p.at[0], mate).wait_send()

    tiles = [(t, min(CH, qw - t * CH)) for t in range((qw + CH - 1) // CH)]

    def use_qkv(j):
        part = u_w.at[j, :, pl.ds(0, qw)]
        pltpu.make_async_copy(part, part, usem.at[j]).wait()
        h = h_all[j].reshape(n_tok, CH)

        @pl.when(j < nch - 1)
        def _():
            for t, n in tiles:
                p = dot(h, u_w[j, :, t * CH:t * CH + n])
                acc[2 * t, :, 0:n] += p[0:st_rows]
                acc[2 * t + 1, :, 0:n] += p[st_rows:]

        @pl.when(j == nch - 1)
        def _():
            for t, n in tiles:
                p = dot(h, u_w[j, :, t * CH:t * CH + n])
                slabs = range(t * CH // hd, (t * CH + n) // hd)
                b = jnp.concatenate([bqkv_ref[s % heads, s // heads:s // heads + 1, :] for s in slabs], axis=1)
                for st in range(2):
                    y = acc[2 * t + st, :, 0:n] + p[st * st_rows:(st + 1) * st_rows]
                    qkv[st * st_rows:(st + 1) * st_rows, t * CH:t * CH + n] = bf16(y + f32(b))
        load_up(j).start()

    for copy in late:
        copy.wait()
    for v in range(GATHER_QKV[0]):
        send_own(piece_both, v)
    with jax.named_scope("gather1"):
        gather(piece_both, all_both, nch, use_qkv, GATHER_QKV)
    def position(i):
        st, s, r, w = i // st_rows, (i // side) % 2, (i // hr) % n_chips, i % hr
        return ((chip + r) % n_chips) * (2 * rows) + (core + s - 2 * core * s) * rows + st * hr + w

    qpos = position(lax.broadcasted_iota(jnp.int32, (n_tok, n_tok), 0))
    kpos = position(lax.broadcasted_iota(jnp.int32, (n_tok, n_tok), 1))
    keep = qpos >= kpos
    for h in range(heads):
        q = qkv[:, h * hd:(h + 1) * hd]
        k = qkv[:, (heads + h) * hd:(heads + h + 1) * hd]
        v = qkv[:, (2 * heads + h) * hd:(2 * heads + h + 1) * hd]
        logits = lax.dot_general(q, k, (((1,), (1,)), ((), ())), preferred_element_type=jnp.float32) * hd ** -0.5
        logits = jnp.where(keep, logits, -1e30)
        e = jnp.exp(logits - jnp.max(logits, axis=1, keepdims=True))
        p = bf16(e / jnp.sum(e, axis=1, keepdims=True))
        ctx[:, h * hd:(h + 1) * hd] = bf16(dot(p, v))

    gather_drain()
    o_all = pool.at[pl.ds(o_base, ng)]
    pltpu.make_async_copy(o_all, o_all, osem).wait()

    def pair_sum(v, st, g):
        for c in range(2):
            j = 2 * g + c
            s = acc[v, c * side:(c + 1) * side, :] + f32(precv[st, j])
            two = bf16(s[2 * hr:3 * hr])
            hop_s[0, st, j] = two[:, 0:hc]
            hop_s[1, st, j] = two[:, hc:]
            acc[v, c * side:(c + 1) * side, :] = s

    def middle_sum(v, st, g):
        for c in range(2):
            j = 2 * g + c
            one = acc[v, c * side + hr:c * side + 2 * hr, :]
            fin_s[0, st, j, :, 0:hc] = bf16(one[:, 0:hc] + f32(hop_r[0, st, j]))
            fin_s[0, st, j, :, hc:] = bf16(one[:, hc:])
            three = acc[v, c * side + 3 * hr:(c + 1) * side, :]
            fin_s[1, st, j, :, 0:hc] = bf16(three[:, 0:hc])
            fin_s[1, st, j, :, hc:] = bf16(three[:, hc:] + f32(hop_r[1, st, j]))

    def fins(st, g, v):
        pair = pl.ds(2 * g, 2)
        return (push(fin_s.at[0, st, pair], fin_r.at[0, st, pair], rs_send, rs_fl.at[v], right),
                push(fin_s.at[1, st, pair], fin_r.at[1, st, pair], rs_send, rs_fr.at[v], left))

    def last_sum(v, st, g, put):
        for copy in fins(st, g, v):
            copy.wait_recv()
        for c in range(2):
            j = 2 * g + c
            total = acc[v, c * side:c * side + hr, :] + f32(fin_r[0, st, j]) + f32(fin_r[1, st, j])
            put(st, j, bf16(xb[st, j] + total))

    def scatter_drain():
        push(psend, precv, rs_send, rs_p.at[0], mate).wait_send()
        push(hop_s, hop_r, rs_send, rs_p.at[0], mate).wait_send()
        push(fin_s, fin_r, rs_send, rs_p.at[0], mate).wait_send()

    bo = f32(bo_ref[...]).reshape(1, dim)
    for j in range(nch):
        cols = slice(j * CH, (j + 1) * CH)
        y = f32(x_ref[:, cols]) + bo[:, cols]
        xb[0, j] = y[0:hr]
        xb[1, j] = y[hr:]

    def pairs_out(g):
        two = pl.ds(2 * g, 2)
        return push(psend.at[:, two], precv.at[:, two], rs_send, rs_p.at[g], mate)

    def hops_out(g):
        two = pl.ds(2 * g, 2)
        return (push(hop_s.at[0, :, two], hop_r.at[0, :, two], rs_send, rs_hl.at[g], right),
                push(hop_s.at[1, :, two], hop_r.at[1, :, two], rs_send, rs_hr.at[g], left))

    def put_x1(st, j, y):
        x1[st, j] = y

    lag_p, lag_h, lag_f = LAGS_OUT

    def out_step(i, carry):
        @pl.when(i < ng)
        def _():
            with jax.named_scope("spart"):
                for c in range(2):
                    j = 2 * i + c
                    p = dot(ctx[...], pool[o_base + i, :, c * CH:(c + 1) * CH])
                    for st in range(2):
                        acc[st * ng + i, c * side:(c + 1) * side, :] = p[st * st_rows:st * st_rows + side]
                        psend[st, j] = bf16(p[st * st_rows + side:(st + 1) * st_rows])
            pairs_out(i).start()

        @pl.when((i >= lag_p) & (i < ng + lag_p))
        def _():
            g = i - lag_p
            with jax.named_scope("swp"):
                pairs_out(g).wait_recv()
            for st in range(2):
                pair_sum(st * ng + g, st, g)
            for copy in hops_out(g):
                copy.start()

        @pl.when((i >= lag_h) & (i < ng + lag_h))
        def _():
            g = i - lag_h
            with jax.named_scope("swh"):
                for copy in hops_out(g):
                    copy.wait_recv()
            for st in range(2):
                middle_sum(st * ng + g, st, g)
            for copy in fins(0, g, g):
                copy.start()

        @pl.when(i == ng + lag_h - 1)
        def _():
            for g in range(ng):
                for copy in fins(1, g, ng + g):
                    copy.start()

        @pl.when(i >= lag_f)
        def _():
            g = i - lag_f
            with jax.named_scope("swf"):
                last_sum(g, 0, g, put_x1)
        return carry

    with jax.named_scope("scatter1"):
        lax.fori_loop(0, ng + lag_f, out_step, 0)

    load_down(N_WD - 1)

    with jax.named_scope("ln2a"):
        norm(lambda j: f32(x1[0, j]), put_stream(0), hr, g2_ref, s2_ref)
    for v in range(GATHER_UP[0]):
        send_own(piece_stream, v)

    def last_out(g, carry):
        last_sum(ng + g, 1, g, put_x1)
        return carry

    with jax.named_scope("last1"):
        lax.fori_loop(0, ng, last_out, 0)
    with jax.named_scope("ln2b"):
        norm(lambda j: f32(x1[1, j]), put_stream(1), hr, g2_ref, s2_ref)
    acc[ng:2 * ng] = jnp.zeros((ng, st_rows, CH), jnp.float32)
    bd = f32(bd_ref[...]).reshape(1, dim)
    for j in range(nch):
        for st in range(2):
            xb[st, j] = f32(x1[st, j]) + bd[:, j * CH:(j + 1) * CH]
    for j in range(nch):
        load_up(j).wait()

    bu = f32(bu_ref[...]).reshape(1, ff)

    def activate(st, t, a):
        cols = slice(t * CH, (t + 1) * CH)
        act[st, :, cols] = bf16(jax.nn.gelu(a + bu[:, cols], approximate=True))

    def use_up(g):
        h = jnp.concatenate([h_all[2 * g, 0], h_all[2 * g + 1, 0]], axis=1)

        def weight(t):
            return u_w[pl.ds(2 * g, 2), :, t * CH:(t + 1) * CH].reshape(2 * CH, CH)

        @pl.when(g < ng - 1)
        def _():
            for t in range(nt):
                acc[ng + t] += dot(h, weight(t))

        @pl.when(g == ng - 1)
        def _():
            for t in range(nt):
                activate(0, t, acc[ng + t] + dot(h, weight(t)))

    def up_whole():
        for g in range(ng):
            wait_mate(all_stream, ng + g)
        with jax.named_scope("muse"):
            h = jnp.concatenate([h_all[j, 1] for j in range(nch)], axis=1)
            for t in range(nt):
                activate(1, t, dot(h, u_w[:, :, t * CH:(t + 1) * CH].reshape(dim, CH)))

    with jax.named_scope("gather2"):
        gather(piece_stream, all_stream, ng, use_up, GATHER_UP)
    scatter_drain()

    def put_out(st, j, y):
        out_ref[pl.ds(pl.multiple_of(st * hr, hr), hr), pl.ds(pl.multiple_of(j * CH, CH), CH)] = y

    def pairs_down(v, st, g):
        two = pl.ds(2 * g, 2)
        return push(psend.at[st, two], precv.at[st, two], rs_send, rs_p.at[v], mate)

    def hops_down(v, st, g):
        two = pl.ds(2 * g, 2)
        return (push(hop_s.at[0, st, two], hop_r.at[0, st, two], rs_send, rs_hl.at[v], right),
                push(hop_s.at[1, st, two], hop_r.at[1, st, two], rs_send, rs_hr.at[v], left))

    def far_down(v, st, g):
        two = pl.ds(2 * g, 2)
        return push(hop_s.at[:, st, two], hop_r.at[:, st, two], rs_send, rs_hl.at[v], far)

    first_far = 2 * ng - N_FAR

    def when_group(k, fn):
        @pl.when((k >= 0) & (k <= 2 * ng) & (k != ng))
        def _():
            st = k // (ng + 1)
            v = k - st
            fn(v, st, v - st * ng)

    lag_p2, lag_h2, lag_f2 = LAGS_DOWN
    done_two = ng + GATHER_UP[2] - GATHER_UP[1]

    def down_part(v, st, g):
        wait_down(v)
        slot = v % N_WD
        with jax.named_scope("dpart"):
            for c in range(2):
                j = 2 * g + c
                p = dot(act[st], pool[pl.ds(slot * nk, nk), :, c * CH:(c + 1) * CH].reshape(ff, CH))
                acc[v, c * side:(c + 1) * side, :] = p[0:side]
                psend[st, j] = bf16(p[side:])

        @pl.when(v + N_WD < 2 * ng)
        def _():
            load_down(v + N_WD)
        pairs_down(v, st, g).start()

    def down_pair(v, st, g):
        with jax.named_scope("dwp"):
            pairs_down(v, st, g).wait_recv()
        pair_sum(v, st, g)

        @pl.when(v < first_far)
        def _():
            for copy in hops_down(v, st, g):
                copy.start()

        @pl.when(v >= first_far)
        def _():
            far_down(v, st, g).start()
            for c in range(2):
                j = 2 * g + c
                fin_s[0, st, j] = bf16(acc[v, c * side + hr:c * side + 2 * hr, :])
                fin_s[1, st, j] = bf16(acc[v, c * side + 3 * hr:(c + 1) * side, :])
            for copy in fins(st, g, v):
                copy.start()

    def down_middle(v, st, g):
        @pl.when(v < first_far)
        def _():
            with jax.named_scope("dwh"):
                for copy in hops_down(v, st, g):
                    copy.wait_recv()
            middle_sum(v, st, g)
            for copy in fins(st, g, v):
                copy.start()

    def down_last(v, st, g):
        @pl.when(v < first_far)
        def _():
            with jax.named_scope("dwf"):
                last_sum(v, st, g, put_out)

        @pl.when(v >= first_far)
        def _():
            with jax.named_scope("dwx"):
                far_down(v, st, g).wait_recv()
                for c in range(2):
                    j = 2 * g + c
                    acc[v, c * side:c * side + hr, 0:hc] += f32(hop_r[0, st, j])
                    acc[v, c * side:c * side + hr, hc:] += f32(hop_r[1, st, j])
                last_sum(v, st, g, put_out)

    def mlp_step(w, carry):
        tail = w >= ng + 1 + lag_h2

        @pl.when(tail)
        def _():
            when_group(w - lag_h2, down_middle)

        when_group(w - lag_p2, down_pair)

        @pl.when(jnp.logical_not(tail))
        def _():
            when_group(w - lag_h2, down_middle)

        when_group(w - lag_f2, down_last)

        @pl.when(w + done_two < nch)
        def _():
            forward_two(piece_stream, w + done_two)

        pl.when(w == ng)(up_whole)
        when_group(w, down_part)
        return carry

    with jax.named_scope("mlp"):
        lax.fori_loop(0, 2 * ng + 1 + lag_f2, mlp_step, 0)
    scatter_drain()
    gather_drain()


def solution(mesh):
    n_dev = mesh.shape["tp"]

    def body(hidden, g1, s1, w_qkv, b_qkv, w_out, b_out, g2, s2, w_up, b_up, w_down, b_down):
        _, rows, dim = hidden.shape
        _, three, heads, hd = w_qkv.shape
        ff = w_up.shape[1]
        nch = dim // CH
        n_tok, hr = rows * n_dev, rows // 2
        st_rows, side = n_tok // 2, n_tok // 4
        bf, fl = jnp.bfloat16, jnp.float32
        row = lambda v: v.reshape(1, -1)
        hbm = pl.BlockSpec(memory_space=pl.ANY)
        dma = pltpu.SemaphoreType.DMA
        out = pl.pallas_call(
            functools.partial(layer_kernel, n_dev),
            out_shape=pltpu.VMEM((rows, dim), bf),
            in_specs=[hbm] * 13,
            out_specs=pl.BlockSpec(memory_space=pltpu.VMEM),
            scratch_shapes=[
                pltpu.VMEM((rows, dim), bf),
                pltpu.VMEM((1, dim), fl), pltpu.VMEM((1, dim), fl),
                pltpu.VMEM((1, dim), fl), pltpu.VMEM((1, dim), fl),
                pltpu.VMEM((heads, three, hd), bf), pltpu.VMEM((dim,), bf),
                pltpu.VMEM((ff,), bf), pltpu.VMEM((dim,), bf),
                pltpu.VMEM((2, nch, hr, CH), fl),
                pltpu.VMEM((nch, 2, st_rows, CH), bf),
                pltpu.VMEM((nch, CH, ff), bf),
                pltpu.VMEM(((N_WD - 1) * (ff // (heads * hd)) + nch // 2, heads * hd, 2 * CH), bf),
                pltpu.VMEM((nch, st_rows, CH), fl),
                pltpu.VMEM((n_tok, three * heads * hd), bf),
                pltpu.VMEM((n_tok, heads * hd), bf),
                pltpu.VMEM((2, st_rows, ff), bf),
                pltpu.VMEM((2, nch, side, CH), bf),
                pltpu.VMEM((2, nch, side, CH), bf),
                pltpu.VMEM((2, 2, nch, hr, CH // 2), bf),
                pltpu.VMEM((2, 2, nch, hr, CH // 2), bf),
                pltpu.VMEM((2, 2, nch, hr, CH), bf),
                pltpu.VMEM((2, 2, nch, hr, CH), bf),
                pltpu.VMEM((2, nch, hr, CH), bf),
                dma((3,)), dma((6,)), dma((nch,)), dma(()), dma((N_WD,)),
                dma(()), dma((nch,)), dma((nch,)), dma((nch,)), dma((nch,)), dma((nch,)),
                dma(()), dma((nch,)), dma((nch,)), dma((nch,)), dma((nch,)), dma((nch,)),
            ],
            compiler_params=pltpu.CompilerParams(
                collective_id=0, has_side_effects=True, vmem_limit_bytes=61 * 1024 * 1024),
            name="decoder_layer",
        )(
            hidden[0], row(g1), row(s1),
            jnp.transpose(w_qkv, (1, 2, 0, 3)).reshape(three * heads, dim, hd),
            jnp.transpose(b_qkv, (1, 0, 2)),
            w_out.reshape(heads * hd, dim), b_out, row(g2), row(s2), w_up, b_up, w_down, b_down,
        )
        return out[None]

    specs = (P("dp", "tp", None), P(), P(), P(None, None, "tp", None), P(None, "tp", None),
             P("tp", None, None), P(), P(), P(), P(None, "tp"), P("tp"), P("tp", None), P())
    return jax.shard_map(body, mesh=mesh, in_specs=specs, out_specs=P("dp", "tp", None), check_vma=False)
```

profile of v0, /device:TPU:81, one launch (start us, length us, event | category | flops | bytes accessed | tf_op | source)
XLA Modules:
  0.0 72.7 jit_solution(6666344125161151503)
XLA Ops:
  0.0 72.0 %decoder_layer.1 = bf16[32,5120]{1,0:T(8,128)(2,1)S(1)} custom-call(bf16[32,5120]{1,0:T(8,128)(2,1)} %bitcast.14, f32[1,5120]{1,0:T(1,128)} %bitcast.15, f32[1,5120]{1,0:T(1,128)} %bitcast.16, bf16[15,5120,128]{2,1,0:T(8,128)(2,1)} %bitcast.12, bf16[5,3,128]{2,1,0:T(4,128)(2,1)} %bitcast.19, bf16[640,5120]{1,0:T(8,128)(2,1)} %bitcast.13, ...), custom_call_target="tpu_custom_call" | custom-call | tf_op jit(solution)/shard_map/decoder_layer/pallas_call | solution.py:559
  72.0 0.7 copy.15
where the time goes:
time: 72.8 us; the launch traced here: 72.7 us
  Pallas kernels  72 us (99%)
  local copies, waits for them, and re-layouts  0.73 us (1%)
    pallas_call x1, Pallas kernels, body(): pl.pallas_call(functools.partial(layer_kernel, n_dev), out_shape=pltpu.VM...  72 us

commit v1 on v0

--- a/solution.py
+++ b/solution.py
@@ -292,6 +292,15 @@
             total = acc[v, c * side:c * side + hr, :] + f32(fin_r[0, st, j]) + f32(fin_r[1, st, j])
             put(st, j, bf16(xb[st, j] + total))
 
+    def pairs_down(v, st, g):
+        two = pl.ds(2 * g, 2)
+        return push(psend.at[st, two], precv.at[st, two], rs_send, rs_p.at[v], mate)
+
+    def hops_down(v, st, g):
+        two = pl.ds(2 * g, 2)
+        return (push(hop_s.at[0, st, two], hop_r.at[0, st, two], rs_send, rs_hl.at[v], right),
+                push(hop_s.at[1, st, two], hop_r.at[1, st, two], rs_send, rs_hr.at[v], left))
+
     def scatter_drain():
         push(psend, precv, rs_send, rs_p.at[0], mate).wait_send()
         push(hop_s, hop_r, rs_send, rs_p.at[0], mate).wait_send()
@@ -307,11 +316,6 @@
     def pairs_out(g):
         two = pl.ds(2 * g, 2)
         return push(psend.at[:, two], precv.at[:, two], rs_send, rs_p.at[g], mate)
-
-    def hops_out(g):
-        two = pl.ds(2 * g, 2)
-        return (push(hop_s.at[0, :, two], hop_r.at[0, :, two], rs_send, rs_hl.at[g], right),
-                push(hop_s.at[1, :, two], hop_r.at[1, :, two], rs_send, rs_hr.at[g], left))
 
     def put_x1(st, j, y):
         x1[st, j] = y
@@ -337,25 +341,28 @@
                 pairs_out(g).wait_recv()
             for st in range(2):
                 pair_sum(st * ng + g, st, g)
-            for copy in hops_out(g):
+            for copy in hops_down(g, 0, g):
                 copy.start()
 
         @pl.when((i >= lag_h) & (i < ng + lag_h))
         def _():
             g = i - lag_h
             with jax.named_scope("swh"):
-                for copy in hops_out(g):
+                for copy in hops_down(g, 0, g):
                     copy.wait_recv()
-            for st in range(2):
-                middle_sum(st * ng + g, st, g)
-            for copy in fins(0, g, g):
+            middle_sum(g, 0, g)
+            for copy in fins(0, g, g) + hops_down(ng + g, 1, g):
                 copy.start()
 
-        @pl.when(i == ng + lag_h - 1)
-        def _():
-            for g in range(ng):
-                for copy in fins(1, g, ng + g):
-                    copy.start()
+        @pl.when((i >= lag_h + ng) & (i < lag_h + 2 * ng))
+        def _():
+            g = i - lag_h - ng
+            with jax.named_scope("swg"):
+                for copy in hops_down(ng + g, 1, g):
+                    copy.wait_recv()
+            middle_sum(ng + g, 1, g)
+            for copy in fins(1, g, ng + g):
+                copy.start()
 
         @pl.when(i >= lag_f)
         def _():
@@ -426,15 +433,6 @@
 
     def put_out(st, j, y):
         out_ref[pl.ds(pl.multiple_of(st * hr, hr), hr), pl.ds(pl.multiple_of(j * CH, CH), CH)] = y
-
-    def pairs_down(v, st, g):
-        two = pl.ds(2 * g, 2)
-        return push(psend.at[st, two], precv.at[st, two], rs_send, rs_p.at[v], mate)
-
-    def hops_down(v, st, g):
-        two = pl.ds(2 * g, 2)
-        return (push(hop_s.at[0, st, two], hop_r.at[0, st, two], rs_send, rs_hl.at[v], right),
-                push(hop_s.at[1, st, two], hop_r.at[1, st, two], rs_send, rs_hr.at[v], left))
 
     def far_down(v, st, g):
         two = pl.ds(2 * g, 2)

time: 72.8 us -> 74.5 us (1.023)
  Pallas kernels: 72 us -> 73.7 us
    pallas_call x1, Pallas kernels: 72 us -> 73.7 us  [body(): pl.pallas_call(functools.partial(layer_kernel, n_dev), out_shape=pltpu.VM...]
where the time goes in v1:
time: 74.5 us; the launch traced here: 74.4 us
  Pallas kernels  73.7 us (99%)
    pallas_call x1, Pallas kernels, body(): pl.pallas_call(functools.partial(layer_kernel, n_dev), out_shape=pltpu.VM...  73.7 us

profile of v1, /device:TPU:81, one launch (start us, length us, event | category | flops | bytes accessed | tf_op | source)
XLA Modules:
  0.0 74.4 jit_solution(16148660488887419404)
XLA Ops:
  0.0 73.7 %decoder_layer.1 = bf16[32,5120]{1,0:T(8,128)(2,1)S(1)} custom-call(bf16[32,5120]{1,0:T(8,128)(2,1)} %bitcast.14, f32[1,5120]{1,0:T(1,128)} %bitcast.15, f32[1,5120]{1,0:T(1,128)} %bitcast.16, bf16[15,5120,128]{2,1,0:T(8,128)(2,1)} %bitcast.12, bf16[5,3,128]{2,1,0:T(4,128)(2,1)} %bitcast.19, bf16[640,5120]{1,0:T(8,128)(2,1)} %bitcast.13, ...), custom_call_target="tpu_custom_call" | custom-call | tf_op jit(solution)/shard_map/decoder_layer/pallas_call | solution.py:557
  73.7 0.7 copy.15

commit v2 on v1

--- a/solution.py
+++ b/solution.py
@@ -11,7 +11,8 @@
 MESH = pl.DeviceIdType.MESH
 CH = 512
 GATHER_QKV = (5, 4, 5)
-GATHER_UP = (5, 4, 5)
+GATHER_UP = (2, 4, 5)
+FIRST_OWN = 5
 LAGS_OUT = (2, 6, 11)
 LAGS_DOWN = (2, 6, 10)
 N_FAR = 1
@@ -177,15 +178,18 @@
             push(at(j, 0, 1, hc, hc), at(j, 0, 2, hc, hc), ag_send, ag_r2.at[j], left).wait_recv()
         push(at(j, 0, 2), at(j, 1, 2), ag_send, ag_p.at[j], mate).start()
 
-    def gather(at, whole, n_use, consume, lags):
+    def gather(at, whole, n_use, consume, lags, between=None):
         look, lag_b, lag_c = lags
 
         def step(i, c):
+            if between is not None:
+                pl.when(i == FIRST_OWN - look)(between)
+
             @pl.when(i < nch)
             def _():
                 forward_one(at, i)
 
-            @pl.when(i + look < nch)
+            @pl.when((i + look >= FIRST_OWN) & (i + look < nch))
             def _():
                 send_own(at, i + look)
 
@@ -235,7 +239,7 @@
 
     for copy in late:
         copy.wait()
-    for v in range(GATHER_QKV[0]):
+    for v in range(FIRST_OWN):
         send_own(piece_both, v)
     with jax.named_scope("gather1"):
         gather(piece_both, all_both, nch, use_qkv, GATHER_QKV)
@@ -378,24 +382,25 @@
 
     with jax.named_scope("ln2a"):
         norm(lambda j: f32(x1[0, j]), put_stream(0), hr, g2_ref, s2_ref)
-    for v in range(GATHER_UP[0]):
+    for v in range(FIRST_OWN):
         send_own(piece_stream, v)
 
     def last_out(g, carry):
         last_sum(ng + g, 1, g, put_x1)
         return carry
 
-    with jax.named_scope("last1"):
-        lax.fori_loop(0, ng, last_out, 0)
-    with jax.named_scope("ln2b"):
-        norm(lambda j: f32(x1[1, j]), put_stream(1), hr, g2_ref, s2_ref)
-    acc[ng:2 * ng] = jnp.zeros((ng, st_rows, CH), jnp.float32)
-    bd = f32(bd_ref[...]).reshape(1, dim)
-    for j in range(nch):
-        for st in range(2):
-            xb[st, j] = f32(x1[st, j]) + bd[:, j * CH:(j + 1) * CH]
-    for j in range(nch):
-        load_up(j).wait()
+    def second_stream():
+        with jax.named_scope("last1"):
+            lax.fori_loop(0, ng, last_out, 0)
+        with jax.named_scope("ln2b"):
+            norm(lambda j: f32(x1[1, j]), put_stream(1), hr, g2_ref, s2_ref)
+        acc[ng:2 * ng] = jnp.zeros((ng, st_rows, CH), jnp.float32)
+        bd = f32(bd_ref[...]).reshape(1, dim)
+        for j in range(nch):
+            for st in range(2):
+                xb[st, j] = f32(x1[st, j]) + bd[:, j * CH:(j + 1) * CH]
+        for j in range(nch):
+            load_up(j).wait()
 
     bu = f32(bu_ref[...]).reshape(1, ff)
 
@@ -428,7 +433,7 @@
                 activate(1, t, dot(h, u_w[:, :, t * CH:(t + 1) * CH].reshape(dim, CH)))
 
     with jax.named_scope("gather2"):
-        gather(piece_stream, all_stream, ng, use_up, GATHER_UP)
+        gather(piece_stream, all_stream, ng, use_up, GATHER_UP, second_stream)
     scatter_drain()
 
     def put_out(st, j, y):

time: 74.5 us -> 78.8 us (1.058)
  Pallas kernels: 73.7 us -> 78 us
    pallas_call x1, Pallas kernels: 73.7 us -> 78 us  [body(): pl.pallas_call(functools.partial(layer_kernel, n_dev), out_shape=pltpu.VM...]
where the time goes in v2:
time: 78.8 us
  Pallas kernels  78 us (99%)
    pallas_call x1, Pallas kernels, body(): pl.pallas_call(functools.partial(layer_kernel, n_dev), out_shape=pltpu.VM...  78 us

profile of v2, /device:TPU:81, one launch (start us, length us, event | category | flops | bytes accessed | tf_op | source)
XLA Modules:
  0.0 78.8 jit_solution(5919105628081209959)
XLA Ops:
  0.0 78.0 %decoder_layer.1 = bf16[32,5120]{1,0:T(8,128)(2,1)S(1)} custom-call(bf16[32,5120]{1,0:T(8,128)(2,1)} %bitcast.14, f32[1,5120]{1,0:T(1,128)} %bitcast.15, f32[1,5120]{1,0:T(1,128)} %bitcast.16, bf16[15,5120,128]{2,1,0:T(8,128)(2,1)} %bitcast.12, bf16[5,3,128]{2,1,0:T(4,128)(2,1)} %bitcast.19, bf16[640,5120]{1,0:T(8,128)(2,1)} %bitcast.13, ...), custom_call_target="tpu_custom_call" | custom-call | tf_op jit(solution)/shard_map/decoder_layer/pallas_call | solution.py:562
  78.0 0.7 copy.15

commit v3 on v0

--- a/solution.py
+++ b/solution.py
@@ -14,7 +14,7 @@
 GATHER_UP = (5, 4, 5)
 LAGS_OUT = (2, 6, 11)
 LAGS_DOWN = (2, 6, 10)
-N_FAR = 1
+N_FAR = 2
 N_WD = 4
 
 

time: 72.8 us -> 73.2 us (level)
  no operation moved by 1% of the time
where the time goes in v3:
time: 73.2 us; the launch traced here: 73.1 us
  Pallas kernels  72.4 us (99%)
    pallas_call x1, Pallas kernels, body(): pl.pallas_call(functools.partial(layer_kernel, n_dev), out_shape=pltpu.VM...  72.4 us

profile of v3, /device:TPU:81, one launch (start us, length us, event | category | flops | bytes accessed | tf_op | source)
XLA Modules:
  0.0 73.1 jit_solution(14252420592267922517)
XLA Ops:
  0.0 72.4 %decoder_layer.1 = bf16[32,5120]{1,0:T(8,128)(2,1)S(1)} custom-call(bf16[32,5120]{1,0:T(8,128)(2,1)} %bitcast.14, f32[1,5120]{1,0:T(1,128)} %bitcast.15, f32[1,5120]{1,0:T(1,128)} %bitcast.16, bf16[15,5120,128]{2,1,0:T(8,128)(2,1)} %bitcast.12, bf16[5,3,128]{2,1,0:T(4,128)(2,1)} %bitcast.19, bf16[640,5120]{1,0:T(8,128)(2,1)} %bitcast.13, ...), custom_call_target="tpu_custom_call" | custom-call | tf_op jit(solution)/shard_map/decoder_layer/pallas_call | solution.py:559
  72.4 0.7 copy.15
